TPU v7x, 32 devices: a whole 2x2x4 slice. The times are simulated.
32 devices in a mesh: band: 8 (over z, y), feat: 4 (over x, core).
Axes of the slice: x: 2, y: 2, z: 4, core: 2. Of those that a mesh axis runs over, the one named last changes fastest.
Arguments:
- grid_latent: bfloat16 [16384, 512], P('band', 'feat'), may hold values from -6 to 6
- mesh_latent: bfloat16 [1280, 512], P('band', 'feat'), may hold values from -6 to 6
- edge_latent: bfloat16 [8, 4, 2048, 512], P('band', 'feat'), may hold values from -6 to 6
- edge_src: int32 [8, 8192], P('band'), may hold values from 0 to 2047
- edge_dst: int32 [8, 4, 2048], P('band', 'feat'), may hold values from 0 to 160, as said below
- edge_w1: bfloat16 [1536, 512], replicated, may hold values from -0.15625 to 0.15625
- edge_b1: float32 [512], replicated, may hold values from -3 to 3
- edge_w2: bfloat16 [512, 512], replicated, may hold values from -0.25 to 0.25
- edge_b2: float32 [512], replicated, may hold values from -2 to 2
- edge_gain: float32 [512], replicated, may hold values from 0.25 to 1.75
- edge_shift: float32 [512], replicated, may hold values from -2 to 2
- node_w1: bfloat16 [1024, 512], replicated, may hold values from -0.1875 to 0.1875
- node_b1: float32 [512], replicated, may hold values from -3 to 3
- node_w2: bfloat16 [512, 512], replicated, may hold values from -0.25 to 0.25
- node_b2: float32 [512], replicated, may hold values from -2 to 2
- node_gain: float32 [512], replicated, may hold values from 0.25 to 1.75
- node_shift: float32 [512], replicated, may hold values from -2 to 2
Outputs:
- mesh_new: bfloat16 [1280, 512], P('band', 'feat')
Inputs may be any that keep to these rules, and one draw needn't show every extreme that they name: `edge_src`: entry [s, d * 1024 + j] is the grid row, counted within band index s, that sends slot j of the edges from band index s to band index d; empty slots hold some row too. `edge_dst`: entry [d, f, s * 256 + q] is the mesh node, counted within band index d, that receives slot f * 256 + q of the edges from band index s to band index d, or 160 where that slot is empty. The used slots of a pair come first; a pair has at most 1024 used slots. Each receiving band index d hears only from the sending band indices of one latitude span of consecutive indices (edges are local), which lies anywhere along band since mesh partitions are face-major; other pairs are empty. In every draw some band indices receive 1024 from every band index of their span.
All inputs are finite; a program needn't handle non-finite values.
Results may differ from a plain program's by a relative error of at most 0.011.
Values may be sent and summed in bfloat16 or wider, within the bound.
A program may use at most 64 MiB of HBM per device.

v0:
```python
import math

import jax
import jax.numpy as jnp
from jax import lax
from jax.sharding import PartitionSpec as P

EPSILON = 1e-05


def normalize(values, norm_gain, norm_shift):
    average = jnp.mean(values, -1, keepdims=True)
    centered = values - average
    variance = jnp.mean(centered * centered, -1, keepdims=True)
    return centered * lax.rsqrt(variance + EPSILON) * norm_gain + norm_shift


def node_step(row_block, summed, node_w1, node_b1, node_w2, node_b2, node_gain, node_shift):
    full_width = row_block.shape[1]
    hidden = jnp.dot(row_block, node_w1[:full_width], preferred_element_type=jnp.float32)
    hidden = (
        hidden
        + jnp.dot(
            summed.astype(jnp.bfloat16), node_w1[full_width:], preferred_element_type=jnp.float32
        )
        + node_b1
    )
    active = jax.nn.silu(hidden).astype(jnp.bfloat16)
    update = jnp.dot(active, node_w2, preferred_element_type=jnp.float32) + node_b2
    return (row_block.astype(jnp.float32) + normalize(update, node_gain, node_shift)).astype(
        jnp.bfloat16
    )


def select_rows(table, indices):
    total = indices.shape[0]
    block_rows = math.gcd(total, 512)
    grouped = indices.reshape(total // block_rows, block_rows)

    def one_block(block_ids):
        row_ids = lax.broadcasted_iota(jnp.int32, (block_rows, table.shape[0]), 1)
        onehot = (row_ids == block_ids[:, None]).astype(table.dtype)
        return jnp.dot(onehot, table, preferred_element_type=jnp.float32).astype(table.dtype)

    return lax.map(one_block, grouped).reshape(total, table.shape[1])


def body(
    grid_latent,
    mesh_latent,
    edge_latent,
    edge_src,
    edge_dst,
    edge_w1,
    edge_b1,
    edge_w2,
    edge_b2,
    edge_gain,
    edge_shift,
    node_w1,
    node_b1,
    node_w2,
    node_b2,
    node_gain,
    node_shift,
):
    band_count = lax.axis_size("band")
    feat_count = lax.axis_size("feat")
    quarter = grid_latent.shape[1]
    full_width = quarter * feat_count
    mesh_count = mesh_latent.shape[0]
    picked = select_rows(grid_latent, edge_src.reshape(-1)).reshape(band_count, -1, quarter)
    regrouped = lax.all_to_all(picked, "feat", split_axis=1, concat_axis=2, tiled=True)
    arrived = lax.all_to_all(regrouped, "band", split_axis=0, concat_axis=0, tiled=True)
    senders = arrived.reshape(-1, full_width)
    own_edges = edge_latent.reshape(-1, full_width)
    targets = edge_dst.reshape(-1)
    recv_weight = edge_w1[2 * full_width :]
    portion = lax.all_gather(mesh_latent, "feat", axis=1, tiled=True)
    projected = jnp.dot(portion, recv_weight, preferred_element_type=jnp.float32)
    node_ids = lax.broadcasted_iota(jnp.int32, (mesh_count, targets.shape[0]), 0)
    clipped = jnp.minimum(targets, mesh_count - 1)
    pick_node = (node_ids == clipped[None, :]).astype(jnp.float32)
    receiver_part = lax.dot_general(
        pick_node,
        projected,
        (((0,), (0,)), ((), ())),
        precision=lax.Precision.HIGHEST,
        preferred_element_type=jnp.float32,
    )
    hidden = jnp.dot(own_edges, edge_w1[:full_width], preferred_element_type=jnp.float32)
    hidden = hidden + jnp.dot(
        senders, edge_w1[full_width : 2 * full_width], preferred_element_type=jnp.float32
    )
    hidden = hidden + receiver_part + edge_b1
    active = jax.nn.silu(hidden).astype(jnp.bfloat16)
    update = jnp.dot(active, edge_w2, preferred_element_type=jnp.float32) + edge_b2
    edge_new = (own_edges.astype(jnp.float32) + normalize(update, edge_gain, edge_shift)).astype(
        jnp.bfloat16
    )
    selector = (node_ids == targets[None, :]).astype(jnp.bfloat16)
    partial_sums = jnp.dot(selector, edge_new, preferred_element_type=jnp.float32)
    summed = lax.psum(partial_sums.astype(jnp.bfloat16), "feat").astype(jnp.float32)
    updated = node_step(portion, summed, node_w1, node_b1, node_w2, node_b2, node_gain, node_shift)
    own_cols = lax.dynamic_slice_in_dim(updated, lax.axis_index("feat") * quarter, quarter, 1)
    return own_cols


def solution(mesh):
    placed = (
        P("band", "feat"),
        P("band", "feat"),
        P("band", "feat", None, None),
        P("band", None),
        P("band", "feat", None),
        P(),
        P(),
        P(),
        P(),
        P(),
        P(),
        P(),
        P(),
        P(),
        P(),
        P(),
        P(),
    )
    return jax.shard_map(
        body, mesh=mesh, in_specs=placed, out_specs=P("band", "feat"), check_vma=False
    )
```

profile of v0, /device:TPU:0, one launch (start us, length us, event | category | flops | bytes accessed | tf_op | source)
XLA Modules:
  0.0 183.7 jit_solution(7006882849579234291)
XLA Ops:
  7.0 1.4 reduce.3
  8.5 31.7 %while.10 = (s32[]{:T(128)}, bf16[16,512,128]{2,1,0:T(8,128)(2,1)S(1)}, s32[16,512]{1,0:T(8,128)S(1)}, bf16[2048,128]{1,0:T(8,128)(2,1)}, s32[]{:T(128)}) while((s32[]{:T(128)}, bf16[16,512,128]{2,1,0:T(8,128)(2,1)S(1)}, s32[16,512]{1,0:T(8,128)S(1)}, bf16[2048,128]{1,0:T(8,128)(2,1)}, s32[]{:T(128)}) %tuple.21), condition=%wide.region_1.2_spmd, body=%wide.region_0.1_spmd.sunk | while | flops 269549568 | bytes 661573 | solution.py:45
  8.5 1.9 %fusion.46 = bf16[16,512,128]{2,1,0:T(8,128)(2,1)S(1)} fusion(bf16[16,512,128]{2,1,0:T(8,128)(2,1)S(1)} %get-tuple-element.73, s32[]{:T(128)} %get-tuple-element.72, bf16[2048,128]{1,0:T(8,128)(2,1)} %get-tuple-element.80, s32[512]{0:T(512)S(1)} %bitcast.39), kind=kOutput, calls=%fused_computation.5.clone.1 | convolution fusion | flops 269549568 | bytes 657412 | tf_op jit(solution)/shard_map/while/body/eval_jaxpr/dot_general | solution.py:43
  10.5 1.9 %fusion.46 = bf16[16,512,128]{2,1,0:T(8,128)(2,1)S(1)} fusion(bf16[16,512,128]{2,1,0:T(8,128)(2,1)S(1)} %get-tuple-element.73, s32[]{:T(128)} %get-tuple-element.72, bf16[2048,128]{1,0:T(8,128)(2,1)} %get-tuple-element.80, s32[512]{0:T(512)S(1)} %bitcast.39), kind=kOutput, calls=%fused_computation.5.clone.1 | convolution fusion | flops 269549568 | bytes 657412 | tf_op jit(solution)/shard_map/while/body/eval_jaxpr/dot_general | solution.py:43
  12.4 1.9 %fusion.46 = bf16[16,512,128]{2,1,0:T(8,128)(2,1)S(1)} fusion(bf16[16,512,128]{2,1,0:T(8,128)(2,1)S(1)} %get-tuple-element.73, s32[]{:T(128)} %get-tuple-element.72, bf16[2048,128]{1,0:T(8,128)(2,1)} %get-tuple-element.80, s32[512]{0:T(512)S(1)} %bitcast.39), kind=kOutput, calls=%fused_computation.5.clone.1 | convolution fusion | flops 269549568 | bytes 657412 | tf_op jit(solution)/shard_map/while/body/eval_jaxpr/dot_general | solution.py:43
  14.4 1.9 %fusion.46 = bf16[16,512,128]{2,1,0:T(8,128)(2,1)S(1)} fusion(bf16[16,512,128]{2,1,0:T(8,128)(2,1)S(1)} %get-tuple-element.73, s32[]{:T(128)} %get-tuple-element.72, bf16[2048,128]{1,0:T(8,128)(2,1)} %get-tuple-element.80, s32[512]{0:T(512)S(1)} %bitcast.39), kind=kOutput, calls=%fused_computation.5.clone.1 | convolution fusion | flops 269549568 | bytes 657412 | tf_op jit(solution)/shard_map/while/body/eval_jaxpr/dot_general | solution.py:43
  16.4 1.9 %fusion.46 = bf16[16,512,128]{2,1,0:T(8,128)(2,1)S(1)} fusion(bf16[16,512,128]{2,1,0:T(8,128)(2,1)S(1)} %get-tuple-element.73, s32[]{:T(128)} %get-tuple-element.72, bf16[2048,128]{1,0:T(8,128)(2,1)} %get-tuple-element.80, s32[512]{0:T(512)S(1)} %bitcast.39), kind=kOutput, calls=%fused_computation.5.clone.1 | convolution fusion | flops 269549568 | bytes 657412 | tf_op jit(solution)/shard_map/while/body/eval_jaxpr/dot_general | solution.py:43
  18.4 1.9 %fusion.46 = bf16[16,512,128]{2,1,0:T(8,128)(2,1)S(1)} fusion(bf16[16,512,128]{2,1,0:T(8,128)(2,1)S(1)} %get-tuple-element.73, s32[]{:T(128)} %get-tuple-element.72, bf16[2048,128]{1,0:T(8,128)(2,1)} %get-tuple-element.80, s32[512]{0:T(512)S(1)} %bitcast.39), kind=kOutput, calls=%fused_computation.5.clone.1 | convolution fusion | flops 269549568 | bytes 657412 | tf_op jit(solution)/shard_map/while/body/eval_jaxpr/dot_general | solution.py:43
  20.4 1.9 %fusion.46 = bf16[16,512,128]{2,1,0:T(8,128)(2,1)S(1)} fusion(bf16[16,512,128]{2,1,0:T(8,128)(2,1)S(1)} %get-tuple-element.73, s32[]{:T(128)} %get-tuple-element.72, bf16[2048,128]{1,0:T(8,128)(2,1)} %get-tuple-element.80, s32[512]{0:T(512)S(1)} %bitcast.39), kind=kOutput, calls=%fused_computation.5.clone.1 | convolution fusion | flops 269549568 | bytes 657412 | tf_op jit(solution)/shard_map/while/body/eval_jaxpr/dot_general | solution.py:43
  22.3 1.9 %fusion.46 = bf16[16,512,128]{2,1,0:T(8,128)(2,1)S(1)} fusion(bf16[16,512,128]{2,1,0:T(8,128)(2,1)S(1)} %get-tuple-element.73, s32[]{:T(128)} %get-tuple-element.72, bf16[2048,128]{1,0:T(8,128)(2,1)} %get-tuple-element.80, s32[512]{0:T(512)S(1)} %bitcast.39), kind=kOutput, calls=%fused_computation.5.clone.1 | convolution fusion | flops 269549568 | bytes 657412 | tf_op jit(solution)/shard_map/while/body/eval_jaxpr/dot_general | solution.py:43
  24.3 1.9 %fusion.46 = bf16[16,512,128]{2,1,0:T(8,128)(2,1)S(1)} fusion(bf16[16,512,128]{2,1,0:T(8,128)(2,1)S(1)} %get-tuple-element.73, s32[]{:T(128)} %get-tuple-element.72, bf16[2048,128]{1,0:T(8,128)(2,1)} %get-tuple-element.80, s32[512]{0:T(512)S(1)} %bitcast.39), kind=kOutput, calls=%fused_computation.5.clone.1 | convolution fusion | flops 269549568 | bytes 657412 | tf_op jit(solution)/shard_map/while/body/eval_jaxpr/dot_general | solution.py:43
  26.3 1.9 %fusion.46 = bf16[16,512,128]{2,1,0:T(8,128)(2,1)S(1)} fusion(bf16[16,512,128]{2,1,0:T(8,128)(2,1)S(1)} %get-tuple-element.73, s32[]{:T(128)} %get-tuple-element.72, bf16[2048,128]{1,0:T(8,128)(2,1)} %get-tuple-element.80, s32[512]{0:T(512)S(1)} %bitcast.39), kind=kOutput, calls=%fused_computation.5.clone.1 | convolution fusion | flops 269549568 | bytes 657412 | tf_op jit(solution)/shard_map/while/body/eval_jaxpr/dot_general | solution.py:43
  28.3 1.9 %fusion.46 = bf16[16,512,128]{2,1,0:T(8,128)(2,1)S(1)} fusion(bf16[16,512,128]{2,1,0:T(8,128)(2,1)S(1)} %get-tuple-element.73, s32[]{:T(128)} %get-tuple-element.72, bf16[2048,128]{1,0:T(8,128)(2,1)} %get-tuple-element.80, s32[512]{0:T(512)S(1)} %bitcast.39), kind=kOutput, calls=%fused_computation.5.clone.1 | convolution fusion | flops 269549568 | bytes 657412 | tf_op jit(solution)/shard_map/while/body/eval_jaxpr/dot_general | solution.py:43
  30.3 1.9 %fusion.46 = bf16[16,512,128]{2,1,0:T(8,128)(2,1)S(1)} fusion(bf16[16,512,128]{2,1,0:T(8,128)(2,1)S(1)} %get-tuple-element.73, s32[]{:T(128)} %get-tuple-element.72, bf16[2048,128]{1,0:T(8,128)(2,1)} %get-tuple-element.80, s32[512]{0:T(512)S(1)} %bitcast.39), kind=kOutput, calls=%fused_computation.5.clone.1 | convolution fusion | flops 269549568 | bytes 657412 | tf_op jit(solution)/shard_map/while/body/eval_jaxpr/dot_general | solution.py:43
  32.2 1.9 %fusion.46 = bf16[16,512,128]{2,1,0:T(8,128)(2,1)S(1)} fusion(bf16[16,512,128]{2,1,0:T(8,128)(2,1)S(1)} %get-tuple-element.73, s32[]{:T(128)} %get-tuple-element.72, bf16[2048,128]{1,0:T(8,128)(2,1)} %get-tuple-element.80, s32[512]{0:T(512)S(1)} %bitcast.39), kind=kOutput, calls=%fused_computation.5.clone.1 | convolution fusion | flops 269549568 | bytes 657412 | tf_op jit(solution)/shard_map/while/body/eval_jaxpr/dot_general | solution.py:43
  34.2 1.9 %fusion.46 = bf16[16,512,128]{2,1,0:T(8,128)(2,1)S(1)} fusion(bf16[16,512,128]{2,1,0:T(8,128)(2,1)S(1)} %get-tuple-element.73, s32[]{:T(128)} %get-tuple-element.72, bf16[2048,128]{1,0:T(8,128)(2,1)} %get-tuple-element.80, s32[512]{0:T(512)S(1)} %bitcast.39), kind=kOutput, calls=%fused_computation.5.clone.1 | convolution fusion | flops 269549568 | bytes 657412 | tf_op jit(solution)/shard_map/while/body/eval_jaxpr/dot_general | solution.py:43
  36.2 1.9 %fusion.46 = bf16[16,512,128]{2,1,0:T(8,128)(2,1)S(1)} fusion(bf16[16,512,128]{2,1,0:T(8,128)(2,1)S(1)} %get-tuple-element.73, s32[]{:T(128)} %get-tuple-element.72, bf16[2048,128]{1,0:T(8,128)(2,1)} %get-tuple-element.80, s32[512]{0:T(512)S(1)} %bitcast.39), kind=kOutput, calls=%fused_computation.5.clone.1 | convolution fusion | flops 269549568 | bytes 657412 | tf_op jit(solution)/shard_map/while/body/eval_jaxpr/dot_general | solution.py:43
  38.2 1.9 %fusion.46 = bf16[16,512,128]{2,1,0:T(8,128)(2,1)S(1)} fusion(bf16[16,512,128]{2,1,0:T(8,128)(2,1)S(1)} %get-tuple-element.73, s32[]{:T(128)} %get-tuple-element.72, bf16[2048,128]{1,0:T(8,128)(2,1)} %get-tuple-element.80, s32[512]{0:T(512)S(1)} %bitcast.39), kind=kOutput, calls=%fused_computation.5.clone.1 | convolution fusion | flops 269549568 | bytes 657412 | tf_op jit(solution)/shard_map/while/body/eval_jaxpr/dot_general | solution.py:43
  41.5 29.8 %all_to_all.23 = bf16[8,1024,128]{2,0,1:T(8,128)(2,1)} all-to-all(bf16[8,1024,128]{2,0,1:T(8,128)(2,1)S(1)} %copy.28), channel_id=1, replica_groups=mesh['band'=8,'feat'=4] {'feat'}, dimensions={1} | all-to-all | bytes 4194304 | tf_op jit(solution)/shard_map/all_to_all | solution.py:73
  71.3 4.5 %copy.30 = bf16[8,256,4,128]{1,3,2,0:T(8,128)(2,1)} copy(bf16[8,256,4,128]{3,0,1,2:T(8,128)(2,1)} %bitcast.37) | data formatting | bytes 4194304 | tf_op jit(solution)/shard_map/all_to_all | solution.py:73
  75.8 6.5 %all-to-all-start.1 = ((bf16[8,256,512]{1,2,0:T(8,128)(2,1)}), bf16[8,256,512]{1,2,0:T(8,128)(2,1)}, u32[]{:S(2)}, u32[]{:S(2)}) async-start(bf16[8,256,512]{1,2,0:T(8,128)(2,1)} %bitcast.36), calls=%async_computation.1 | async-start | bytes 4194304 | tf_op jit(solution)/shard_map/all_to_all | solution.py:74
  82.3 2.5 %copy.27 = bf16[1,1,2048,512]{2,3,1,0:T(8,128)(2,1)} copy(bf16[1,1,2048,512]{3,2,1,0:T(8,128)(2,1)S(1)} %copy-done.1) | data formatting | bytes 4194304 | tf_op args[2]
  84.8 5.7 %all_gather.3 = bf16[160,512]{1,0:T(8,128)(2,1)S(1)} all-gather(bf16[160,128]{1,0:T(8,128)(2,1)S(1)} %copy-done.5), channel_id=1, replica_groups=mesh['band'=8,'feat'=4] {'feat'}, dimensions={1}, use_global_device_ids=true | all-gather | bytes 204800 | tf_op jit(solution)/shard_map/all_gather | solution.py:79
  91.8 4.2 %fusion.5 = f32[2048,512]{1,0:T(8,128)} fusion(bf16[1,1,2048,512]{3,2,1,0:T(8,128)(2,1)S(1)} %copy-done.1, bf16[1536,512]{1,0:T(8,128)(2,1)} %param.24), kind=kOutput, calls=%fused_computation.11 | convolution fusion | flops 1073741824 | bytes 6815744 | tf_op jit(solution)/shard_map/dot_general | solution.py:91
  96.1 34.2 %all-to-all-done.1 = bf16[8,256,512]{1,2,0:T(8,128)(2,1)} async-done(((bf16[8,256,512]{1,2,0:T(8,128)(2,1)}), bf16[8,256,512]{1,2,0:T(8,128)(2,1)}, u32[]{:S(2)}, u32[]{:S(2)}) %all-to-all-start.1) | async-done | bytes 2097184 | tf_op jit(solution)/shard_map/all_to_all | solution.py:74
  130.3 2.9 %copy.31 = bf16[8,256,512]{2,1,0:T(8,128)(2,1)S(1)} copy(bf16[8,256,512]{1,2,0:T(8,128)(2,1)} %all-to-all-done.1) | data formatting | bytes 4194304 | tf_op jit(solution)/shard_map/all_to_all | solution.py:74
  133.2 2.4 %fusion.15 = f32[2048,512]{1,0:T(8,128)S(1)} fusion(bf16[2048,512]{1,0:T(8,128)(2,1)S(1)} %bitcast.35, bf16[1536,512]{1,0:T(8,128)(2,1)} %param.24), kind=kOutput, calls=%fused_computation.25 | convolution fusion | flops 1073741824 | bytes 6815744 | tf_op jit(solution)/shard_map/dot_general | solution.py:92
  135.6 3.0 %multiply_convert_fusion = bf16[2048,512]{1,0:T(8,128)(2,1)S(1)} fusion(f32[2048,512]{1,0:T(8,128)S(1)} %copy-done.2, f32[2048,512]{1,0:T(8,128)S(1)} %fusion.15, f32[160,512]{1,0:T(8,128)S(1)} %fusion.13, f32[512]{0:T(512)S(1)} %copy-done.9, s32[2048]{0:T(1024)S(1)} %broadcast_minimum_fusion), kind=kOutput, calls=%fused_computation.9 | convolution fusion | flops 2021982208 | bytes 10823680 | tf_op jit(solution)/shard_map/dot_general | solution.py:84
  138.7 1.4 add_reduce_fusion
  141.7 2.3 %fusion.9 = bf16[160,512]{1,0:T(8,128)(2,1)} fusion(f32[2048,512]{0,1:T(8,128)S(1)} %get-tuple-element.39, bf16[1,1,2048,512]{2,3,1,0:T(8,128)(2,1)S(1)} %copy-done.3, f32[512]{0:T(512)S(1)} %copy-done.10, f32[512]{0:T(512)S(1)} %copy-done.11, f32[2048]{0:T(1024)S(1)} %add_rsqrt_fusion, f32[2048]{0:T(1024)S(1)} %broadcast_multiply_fusion, ...), kind=kOutput, calls=%fused_computation.19 | convolution fusion | flops 344342528 | bytes 6486016 | tf_op jit(solution)/shard_map/dot_general | solution.py:102
  145.7 28.6 %all-reduce.2.cloned.1.call-done = bf16[160,512]{1,0:T(8,128)(2,1)} async-done(((bf16[160,512]{1,0:T(8,128)(2,1)}), bf16[160,512]{1,0:T(8,128)(2,1)}) %all-reduce.2.cloned.1.call-update) | async-done | bytes 163856 | tf_op jit(solution)/shard_map/psum | solution.py:103
  174.4 1.5 fusion.31
  (62 shorter events, 7.7 us)
Async XLA Ops:
  6.5 132.1 %copy-start = (bf16[512,512]{1,0:T(8,128)(2,1)S(1)}, bf16[512,512]{1,0:T(8,128)(2,1)}, u32[]{:S(2)}) copy-start(bf16[512,512]{1,0:T(8,128)(2,1)} %param.26) | copy-start | bytes 1572868
  71.3 11.0 %copy-start.1 = (bf16[1,1,2048,512]{3,2,1,0:T(8,128)(2,1)S(1)}, bf16[1,1,2048,512]{3,2,1,0:T(8,128)(2,1)}, u32[]{:S(2)}) copy-start(bf16[1,1,2048,512]{3,2,1,0:T(8,128)(2,1)} %param.21) | copy-start | bytes 6291460
  75.8 9.1 %copy-start.5 = (bf16[160,128]{1,0:T(8,128)(2,1)S(1)}, bf16[160,128]{1,0:T(8,128)(2,1)}, u32[]{:S(2)}) copy-start(bf16[160,128]{1,0:T(8,128)(2,1)} %param.20) | copy-start | bytes 122884
  75.8 14.8 %copy-start.6 = (s32[1,1,2048]{2,1,0:T(1,128)S(1)}, s32[1,1,2048]{2,1,0:T(1,128)}, u32[]{:S(2)}) copy-start(s32[1,1,2048]{2,1,0:T(1,128)} %param.23) | copy-start | bytes 24580
  75.8 54.5 %all-to-all-start.1 = ((bf16[8,256,512]{1,2,0:T(8,128)(2,1)}), bf16[8,256,512]{1,2,0:T(8,128)(2,1)}, u32[]{:S(2)}, u32[]{:S(2)}) async-start(bf16[8,256,512]{1,2,0:T(8,128)(2,1)} %bitcast.36), calls=%async_computation.1 | async-start | bytes 4194304 | tf_op jit(solution)/shard_map/all_to_all | solution.py:74
  82.3 92.1 %all-reduce.2.cloned.1.call-start = ((), (), s32[]{:S(2)}) async-start(), calls=%async_computation.2 | async-start | bytes 327680 | tf_op jit(solution)/shard_map/psum | solution.py:103
  133.1 2.5 %copy-start.2 = (f32[2048,512]{1,0:T(8,128)S(1)}, f32[2048,512]{1,0:T(8,128)}, u32[]{:S(2)}) copy-start(f32[2048,512]{1,0:T(8,128)} %fusion.5) | copy-start | bytes 12582916
  133.1 2.5 %copy-start.9 = (f32[512]{0:T(512)S(1)}, f32[512]{0:T(512)}, u32[]{:S(2)}) copy-start(f32[512]{0:T(512)} %param.25) | copy-start | bytes 6148
  135.6 3.0 %copy-start.7 = (f32[512]{0:T(512)S(1)}, f32[512]{0:T(512)}, u32[]{:S(2)}) copy-start(f32[512]{0:T(512)} %param.27) | copy-start | bytes 6148
  140.0 1.6 copy-start.3
  140.1 1.6 copy-start.10
  140.1 1.6 copy-start.11
  141.6 2.3 %copy-start.4 = (bf16[1024,512]{1,0:T(8,128)(2,1)S(1)}, bf16[1024,512]{1,0:T(8,128)(2,1)}, u32[]{:S(2)}) copy-start(bf16[1024,512]{1,0:T(8,128)(2,1)} %param.30) | copy-start | bytes 3145732
  141.6 32.7 %copy-start.8 = (bf16[512,512]{1,0:T(8,128)(2,1)S(1)}, bf16[512,512]{1,0:T(8,128)(2,1)}, u32[]{:S(2)}) copy-start(bf16[512,512]{1,0:T(8,128)(2,1)} %param.32) | copy-start | bytes 1572868
  141.6 32.7 %copy-start.12 = (f32[512]{0:T(512)S(1)}, f32[512]{0:T(512)}, u32[]{:S(2)}) copy-start(f32[512]{0:T(512)} %param.33) | copy-start | bytes 6148
  141.7 32.7 %copy-start.13 = (f32[512]{0:T(512)S(1)}, f32[512]{0:T(512)}, u32[]{:S(2)}) copy-start(f32[512]{0:T(512)} %param.31) | copy-start | bytes 6148
Sparse Core Ops, SparseCore 0:
  144.1 30.2 all-reduce.1
where the time goes:
time: 185 us; the launch traced here: 184 us
  waiting for transfers between devices  62.9 us (34%)
  matrix products  47.5 us (26%)
  blocking collectives  35.5 us (19%)
  local copies, waits for them, and re-layouts  14.3 us (8%)
  between operations  13.6 us (7%)
  starting transfers between devices  6.57 us (4%)
  other arithmetic  2.98 us (2%)
    all_to_all x1, waiting for transfers between devices, body(): lax.all_to_all(regrouped, 'band', split_axis=0, concat_axis=0, tiled=True)  34.2 us
    dot_general x16, matrix products, one_block(): jnp.dot(onehot, table, preferred_element_type=jnp.float32)  31.1 us
    all_to_all x1, blocking collectives, body(): lax.all_to_all(picked, 'feat', split_axis=1, concat_axis=2, tiled=True)  29.8 us
    psum x1, waiting for transfers between devices, body(): lax.psum(partial_sums.astype(jnp.bfloat16), 'feat').astype(jnp.float32)  28.6 us
    all_to_all x1, starting transfers between devices, body(): lax.all_to_all(regrouped, 'band', split_axis=0, concat_axis=0, tiled=True)  6.53 us
    all_gather x1, blocking collectives, body(): portion = lax.all_gather(mesh_latent, 'feat', axis=1, tiled=True)  5.7 us
    all_to_all x1, local copies, waits for them, and re-layouts, body(): lax.all_to_all(picked, 'feat', split_axis=1, concat_axis=2, tiled=True)  4.46 us
    dot_general x1, matrix products, body(): jnp.dot(own_edges, edge_w1[:full_width], preferred_element_type=jnp.float32)  4.22 us
  transfers between devices with their start and end apart: 2, of which 2 were waited for; matrix products, arithmetic and copies ran while one was open for 5% of the time, Pallas kernels for 0%

commit v1 on v0

v1 whole, which is shorter than its diff:
```python
import functools

import jax
import jax.numpy as jnp
from jax import lax
from jax.experimental import pallas as pl
from jax.experimental.pallas import tpu as pltpu
from jax.sharding import PartitionSpec as P

EPSILON = 1e-05
LANES = 128
CHUNKS = 4
MESH = pl.DeviceIdType.MESH
F32 = jnp.float32
BF16 = jnp.bfloat16


def normalize(values, norm_gain, norm_shift):
    average = jnp.mean(values, -1, keepdims=True)
    centered = values - average
    variance = jnp.mean(centered * centered, -1, keepdims=True)
    return centered * lax.rsqrt(variance + EPSILON) * norm_gain + norm_shift


def silu(v):
    half = 0.5 * v
    return half + half * jnp.tanh(half)


def dot(a, b):
    return jnp.dot(a, b, preferred_element_type=F32)


def columns(row):
    return jnp.broadcast_to(row, (LANES, LANES)).T


def kernel(
    n,
    nf,
    grid_ref,
    mesh_ref,
    src_ref,
    dst_ref,
    dst_wide,
    vec_ref,
    edge_hbm,
    w1_hbm,
    w2_hbm,
    nw1_hbm,
    nw2_hbm,
    out_ref,
    edge,
    w1,
    w2,
    nw1,
    nw2,
    table,
    nodes,
    onehot,
    outgoing,
    arrived,
    base,
    mesh_full,
    total,
    parts,
    part_in,
    cols_out,
    cols_in,
    local_sem,
    mesh_send,
    mesh_recv,
    core_sem,
    x_send,
    x_recv,
    fwd_send,
    fwd_recv,
    band_send,
    band_recv,
    sum_send,
    sum_recv,
    out_send,
    out_recv,
):
    b = lax.axis_index("band")
    f = lax.axis_index("feat")
    grid_rows = grid_ref.shape[0]
    quarter = grid_ref.shape[1]
    width = quarter * nf
    slots = edge.shape[0]
    quart = slots // n
    mesh_rows = mesh_ref.shape[0]
    own_rows = mesh_rows // nf
    pair = 2 * quarter
    h = f // 2
    c = lax.rem(f, 2)
    core_peer = h * 2 + (1 - c)
    x_peer = (1 - h) * 2 + c

    loads = [
        pltpu.make_async_copy(a, v, local_sem.at[i])
        for i, (a, v) in enumerate(
            ((w1_hbm, w1), (edge_hbm, edge), (w2_hbm, w2), (nw1_hbm, nw1), (nw2_hbm, nw2))
        )
    ]
    for load in loads:
        load.start()

    barrier = pltpu.get_barrier_semaphore()
    for k in range(1, nf):
        pl.semaphore_signal(barrier, inc=1, device_id=(b, lax.rem(f + k, nf)), device_id_type=MESH)
    for k in range(1, n):
        pl.semaphore_signal(barrier, inc=1, device_id=(lax.rem(b + k, n), f), device_id_type=MESH)
    pl.semaphore_wait(barrier, nf - 1 + n - 1)

    def remote(src, dst, send, recv, band, feat):
        return pltpu.make_async_remote_copy(
            src_ref=src,
            dst_ref=dst,
            send_sem=send,
            recv_sem=recv,
            device_id=(band, feat),
            device_id_type=MESH,
        )

    def cols(i):
        return pl.ds(pl.multiple_of(i * quarter, quarter), quarter)

    step = grid_rows // CHUNKS

    def x_copy(i):
        rows = pl.ds(i * step, step)
        return remote(
            grid_ref.at[rows, :], table.at[h, rows, cols(c)], x_send.at[i], x_recv.at[i], b, x_peer
        )

    def fwd_copy(i):
        rows = pl.ds(i * step, step)
        place = table.at[1 - h, rows, cols(c)]
        return remote(place, place, fwd_send.at[i], fwd_recv.at[i], b, core_peer)

    core_copy = remote(
        grid_ref, table.at[h, :, cols(c)], core_sem.at[0], core_sem.at[1], b, core_peer
    )
    mesh_copies = [
        remote(mesh_ref, nodes.at[f], mesh_send.at[k - 1], mesh_recv.at[k - 1], b, lax.rem(f + k, nf))
        for k in range(1, nf)
    ]
    core_copy.start()
    x_copies = [x_copy(i) for i in range(CHUNKS)]
    for copy in x_copies:
        copy.start()
    for copy in mesh_copies:
        copy.start()

    nodes[f] = mesh_ref[...]
    table[h, :, cols(c)] = grid_ref[...]

    lane = lax.broadcasted_iota(jnp.int32, (LANES, LANES), 1)

    def build(t, carry):
        ids = columns(src_ref[pl.ds(t, 1), :])
        rows = pl.ds(pl.multiple_of(t * LANES, LANES), LANES)
        for k in range(grid_rows // LANES):
            hit = jnp.where(lane + k * LANES == ids, 1.0, 0.0)
            onehot[rows, k * LANES : (k + 1) * LANES] = hit.astype(BF16)
        return carry

    lax.fori_loop(0, slots // LANES, build, 0)
    core_copy.wait_recv()

    def band_copy(j, o):
        d = lax.rem(b + o, n)
        return remote(
            outgoing.at[j, o],
            arrived.at[j, b],
            band_send.at[j, o],
            band_recv.at[j, o],
            d,
            f,
        )

    def gather(j, half):
        def piece(o):
            d = lax.rem(b + o, n)
            rows = pl.ds(pl.multiple_of(d * quart, quart), quart)
            return dot(onehot[rows, :], table[half]).astype(BF16)

        def one(o, carry):
            outgoing[j, o] = piece(o)

            @pl.when(o > 1)
            def _():
                band_copy(j, o - 1).start()

            return carry

        lax.fori_loop(1, n, one, 0)
        arrived[j, b] = piece(0)
        band_copy(j, n - 1).start()

    gather(0, h)

    for load in loads[:2]:
        load.wait()
    for copy in mesh_copies:
        copy.wait_recv()
    mesh_wide = jnp.concatenate([nodes[k] for k in range(nf)], axis=1)
    mesh_full[...] = mesh_wide.astype(F32)
    block = 2 * LANES
    node_lane = lax.broadcasted_iota(jnp.int32, (LANES, mesh_rows), 1)
    b1 = vec_ref[0:1, :]

    def prepare(t, carry):
        picks = []
        for i in range(2):
            ids = columns(dst_wide[pl.ds(2 * t + i, 1), :])
            ids = jnp.minimum(ids, mesh_rows - 1)
            spread = jnp.concatenate([ids] * ((mesh_rows + LANES - 1) // LANES), axis=1)[:, :mesh_rows]
            hit = jnp.where(node_lane == spread, 1.0, 0.0).astype(BF16)
            picks.append(dot(hit, mesh_wide_ref()).astype(BF16))
        receivers = jnp.concatenate(picks, axis=0)
        rows = pl.ds(pl.multiple_of(t * block, block), block)
        base[rows, :] = (
            dot(edge[rows, :], w1[:width, :]) + dot(receivers, w1[2 * width :, :]) + b1
        )
        return carry

    def mesh_wide_ref():
        return jnp.concatenate([nodes[k] for k in range(nf)], axis=1)

    lax.fori_loop(0, slots // block, prepare, 0)
    for load in loads[2:]:
        load.wait()
    my_nodes = pl.ds(pl.multiple_of(f * own_rows, 8), own_rows)
    my_mesh = mesh_full[my_nodes, :]
    node_base = dot(my_mesh.astype(BF16), nw1[:width, :]) + vec_ref[4:5, :]

    fwd_copies = [fwd_copy(i) for i in range(CHUNKS)]
    for i in range(CHUNKS):
        x_copies[i].wait_recv()
        fwd_copies[i].start()
    for copy in fwd_copies:
        copy.wait_recv()
    gather(1, 1 - h)

    b2 = vec_ref[1:2, :]
    gain = vec_ref[2:3, :]
    shift = vec_ref[3:4, :]
    total[...] = jnp.zeros_like(total)
    node_row = lax.broadcasted_iota(jnp.int32, (mesh_rows, quart), 0)

    def edges(o, carry):
        s = lax.rem(b - o + n, n)

        @pl.when(o > 0)
        def _():
            band_copy(0, o).wait_recv()
            band_copy(1, o).wait_recv()

        rows = pl.ds(pl.multiple_of(s * quart, quart), quart)
        low = pl.ds(pl.multiple_of(width + h * pair, pair), pair)
        high = pl.ds(pl.multiple_of(width + (1 - h) * pair, pair), pair)
        hidden = base[rows, :] + dot(arrived[0, s], w1[low, :]) + dot(arrived[1, s], w1[high, :])
        update = dot(silu(hidden).astype(BF16), w2[...]) + b2
        fresh = (edge[rows, :].astype(F32) + normalize(update, gain, shift)).astype(BF16)
        hit = jnp.where(node_row == dst_ref[pl.ds(s, 1), :], 1.0, 0.0).astype(BF16)
        total[...] += dot(hit, fresh)
        return carry

    lax.fori_loop(0, n, edges, 0)

    for k in range(nf):
        parts[k] = total[k * own_rows : (k + 1) * own_rows, :].astype(BF16)
    sum_copies = []
    for k in range(1, nf):
        p = lax.rem(f + k, nf)
        sum_copies.append(
            remote(parts.at[p], part_in.at[k - 1], sum_send.at[k - 1], sum_recv.at[k - 1], b, p)
        )
    for copy in sum_copies:
        copy.start()
    summed = parts[f].astype(F32)
    for k in range(1, nf):
        sum_copies[k - 1].wait_recv()
        summed = summed + part_in[k - 1].astype(F32)
    hidden = node_base + dot(summed.astype(BF16), nw1[width:, :])
    update = dot(silu(hidden).astype(BF16), nw2[...]) + vec_ref[5:6, :]
    fresh = (my_mesh + normalize(update, vec_ref[6:7, :], vec_ref[7:8, :])).astype(BF16)
    for k in range(nf):
        cols_out[k] = fresh[:, k * quarter : (k + 1) * quarter]
    out_copies = []
    for k in range(1, nf):
        p = lax.rem(f + k, nf)
        out_copies.append(
            remote(cols_out.at[p], cols_in.at[f], out_send.at[k - 1], out_recv.at[k - 1], b, p)
        )
    for copy in out_copies:
        copy.start()
    cols_in[f] = cols_out[f]
    for copy in out_copies:
        copy.wait_recv()
    out_ref[...] = jnp.concatenate([cols_in[k].astype(F32) for k in range(nf)], axis=0).astype(BF16)

    core_copy.wait_send()
    for copy in x_copies + mesh_copies + fwd_copies + sum_copies + out_copies:
        copy.wait_send()

    def drain(o, carry):
        band_copy(0, o).wait_send()
        band_copy(1, o).wait_send()
        return carry

    lax.fori_loop(1, n, drain, 0)


def body(
    grid_latent,
    mesh_latent,
    edge_latent,
    edge_src,
    edge_dst,
    edge_w1,
    edge_b1,
    edge_w2,
    edge_b2,
    edge_gain,
    edge_shift,
    node_w1,
    node_b1,
    node_w2,
    node_b2,
    node_gain,
    node_shift,
):
    n = lax.axis_size("band")
    nf = lax.axis_size("feat")
    grid_rows, quarter = grid_latent.shape
    width = quarter * nf
    mesh_rows = mesh_latent.shape[0]
    own_rows = mesh_rows // nf
    edges = edge_latent.reshape(-1, width)
    slots = edges.shape[0]
    quart = slots // n
    hidden = edge_w1.shape[1]
    own_src = lax.dynamic_slice_in_dim(
        edge_src.reshape(n, nf, quart), lax.axis_index("feat"), 1, 1
    ).reshape(-1, LANES)
    vectors = jnp.stack(
        [edge_b1, edge_b2, edge_gain, edge_shift, node_b1, node_b2, node_gain, node_shift]
    )
    vmem = pl.BlockSpec(memory_space=pltpu.VMEM)
    anyspace = pl.BlockSpec(memory_space=pl.ANY)
    dma = pltpu.SemaphoreType.DMA
    return pl.pallas_call(
        functools.partial(kernel, n, nf),
        out_shape=jax.ShapeDtypeStruct((mesh_rows, quarter), BF16),
        in_specs=[vmem] * 6 + [anyspace] * 5,
        out_specs=vmem,
        scratch_shapes=[
            pltpu.VMEM((slots, width), BF16),
            pltpu.VMEM(edge_w1.shape, BF16),
            pltpu.VMEM(edge_w2.shape, BF16),
            pltpu.VMEM(node_w1.shape, BF16),
            pltpu.VMEM(node_w2.shape, BF16),
            pltpu.VMEM((nf // 2, grid_rows, 2 * quarter), BF16),
            pltpu.VMEM((nf, mesh_rows, quarter), BF16),
            pltpu.VMEM((slots, grid_rows), BF16),
            pltpu.VMEM((2, n, quart, 2 * quarter), BF16),
            pltpu.VMEM((2, n, quart, 2 * quarter), BF16),
            pltpu.VMEM((slots, hidden), F32),
            pltpu.VMEM((mesh_rows, width), F32),
            pltpu.VMEM((mesh_rows, width), F32),
            pltpu.VMEM((nf, own_rows, width), BF16),
            pltpu.VMEM((nf - 1, own_rows, width), BF16),
            pltpu.VMEM((nf, own_rows, quarter), BF16),
            pltpu.VMEM((nf, own_rows, quarter), BF16),
            dma((5,)),
            dma((nf - 1,)),
            dma((nf - 1,)),
            dma((2,)),
            dma((CHUNKS,)),
            dma((CHUNKS,)),
            dma((CHUNKS,)),
            dma((CHUNKS,)),
            dma((2, n)),
            dma((2, n)),
            dma((nf - 1,)),
            dma((nf - 1,)),
            dma((nf - 1,)),
            dma((nf - 1,)),
        ],
        compiler_params=pltpu.CompilerParams(
            collective_id=0, has_side_effects=True, vmem_limit_bytes=56 * 1024 * 1024
        ),
        name="encoder_step",
    )(
        grid_latent,
        mesh_latent,
        own_src,
        edge_dst.reshape(n, quart),
        edge_dst.reshape(-1, LANES),
        vectors,
        edges,
        edge_w1,
        edge_w2,
        node_w1,
        node_w2,
    )


def solution(mesh):
    placed = (
        P("band", "feat"),
        P("band", "feat"),
        P("band", "feat", None, None),
        P("band", None),
        P("band", "feat", None),
    ) + (P(),) * 12
    return jax.shard_map(
        body, mesh=mesh, in_specs=placed, out_specs=P("band", "feat"), check_vma=False
    )
```

time: 185 us -> 72.9 us (0.39)
  the two profiles are of different devices: /device:TPU:0 before, /device:TPU:29 now
where the time goes in v1:
time: 72.9 us; the launch traced here: 72.5 us
  Pallas kernels  65.1 us (89%)
  local copies, waits for them, and re-layouts  4.56 us (6%)
  other arithmetic  2.84 us (4%)
    pallas_call x1, Pallas kernels, body(): pl.pallas_call(functools.partial(kernel, n, nf), out_shape=jax.ShapeDtype...  65.1 us
    unnamed x2, other arithmetic  2.84 us
    unnamed x2, local copies, waits for them, and re-layouts  1.91 us

profile of v1, /device:TPU:29, one launch (start us, length us, event | category | flops | bytes accessed | tf_op | source)
XLA Modules:
  0.0 72.5 jit_solution(15331056866634351250)
XLA Ops:
  0.0 0.5 broadcast.6
  0.5 1.5 %reduce.6 = s32[8192]{0:T(1024)S(1)} reduce(s32[1,8192]{1,0:T(1,128)} %param.20, s32[]{:T(128)} %broadcast.6), dimensions={0}, to_apply=%param.20.reduce_sub_computation.3 | reduce | bytes 65540 | tf_op args[3]
  2.0 0.6 constant_dynamic-slice_fusion
  2.6 1.4 %reduce.7 = s32[2048]{0:T(1024)S(1)} reduce(s32[1,1,2048]{2,1,0:T(1,128)} %param.21, s32[]{:T(128)} %broadcast.6), dimensions={0,1}, to_apply=%param.21.reduce_sub_computation.3 | reduce | bytes 16388 | tf_op args[4]
  4.0 0.6 reshape.17.dst_ref
  4.6 1.4 %stack.35.vec_ref = f32[8,512]{1,0:T(8,128)} concatenate(f32[1,512]{1,0:T(1,128)} %bitcast.14, f32[1,512]{1,0:T(1,128)} %bitcast.15, f32[1,512]{1,0:T(1,128)} %bitcast.16, f32[1,512]{1,0:T(1,128)} %bitcast.17, f32[1,512]{1,0:T(1,128)} %bitcast.18, f32[1,512]{1,0:T(1,128)} %bitcast.19, f32[1,512]{1,0:T(1,128)} %bitcast.20, f32[1,512]{1,0:T(1,128)} %bitcast.21), dimensions={0} | concatenate | bytes 32768 | tf_op jit(solution)/shard_map/stack | solution.py:349
  6.0 65.1 %encoder_step.1 = bf16[160,128]{1,0:T(8,128)(2,1)} custom-call(bf16[2048,128]{1,0:T(8,128)(2,1)} %grid_ref.1, bf16[160,128]{1,0:T(8,128)(2,1)} %mesh_ref.1, s32[16,128]{1,0:T(8,128)} %bitcast.13, s32[8,256]{1,0:T(8,128)} %reshape.17.dst_ref, s32[16,128]{1,0:T(8,128)} %bitcast.12, f32[8,512]{1,0:T(8,128)} %stack.35.vec_ref, bf16[2048,512]{1,0:T(8,128)(2,1)} %bitcast.11, ...), custom_call_target="tpu_custom_call" | custom-call | tf_op jit(solution)/shard_map/encoder_step/pallas_call | solution.py:355
  71.1 1.4 %copy.21 = bf16[160,128]{1,0:T(8,128)(2,1)} copy(bf16[160,128]{1,0:T(8,128)(2,1)} %encoder_step.1) | data formatting | bytes 81920
  (1 shorter events, 0.0 us)

commit v2 on v1

--- a/solution.py
+++ b/solution.py
@@ -43,7 +43,14 @@
     src_ref,
     dst_ref,
     dst_wide,
-    vec_ref,
+    b1_ref,
+    b2_ref,
+    gain_ref,
+    shift_ref,
+    nb1_ref,
+    nb2_ref,
+    ngain_ref,
+    nshift_ref,
     edge_hbm,
     w1_hbm,
     w2_hbm,
@@ -89,6 +96,7 @@
     width = quarter * nf
     slots = edge.shape[0]
     quart = slots // n
+    aligned = quart % LANES == 0
     mesh_rows = mesh_ref.shape[0]
     own_rows = mesh_rows // nf
     pair = 2 * quarter
@@ -159,7 +167,12 @@
     lane = lax.broadcasted_iota(jnp.int32, (LANES, LANES), 1)
 
     def build(t, carry):
-        ids = columns(src_ref[pl.ds(t, 1), :])
+        if aligned:
+            per = quart // LANES
+            at = (t // per) * (nf * quart) + f * quart + lax.rem(t, per) * LANES
+        else:
+            at = t * LANES
+        ids = columns(src_ref[:, pl.ds(pl.multiple_of(at, LANES), LANES)])
         rows = pl.ds(pl.multiple_of(t * LANES, LANES), LANES)
         for k in range(grid_rows // LANES):
             hit = jnp.where(lane + k * LANES == ids, 1.0, 0.0)
@@ -209,12 +222,13 @@
     mesh_full[...] = mesh_wide.astype(F32)
     block = 2 * LANES
     node_lane = lax.broadcasted_iota(jnp.int32, (LANES, mesh_rows), 1)
-    b1 = vec_ref[0:1, :]
+    b1 = b1_ref[...]
 
     def prepare(t, carry):
         picks = []
         for i in range(2):
-            ids = columns(dst_wide[pl.ds(2 * t + i, 1), :])
+            at = pl.multiple_of((2 * t + i) * LANES, LANES)
+            ids = columns(dst_wide[:, pl.ds(at, LANES)])
             ids = jnp.minimum(ids, mesh_rows - 1)
             spread = jnp.concatenate([ids] * ((mesh_rows + LANES - 1) // LANES), axis=1)[:, :mesh_rows]
             hit = jnp.where(node_lane == spread, 1.0, 0.0).astype(BF16)
@@ -234,7 +248,7 @@
         load.wait()
     my_nodes = pl.ds(pl.multiple_of(f * own_rows, 8), own_rows)
     my_mesh = mesh_full[my_nodes, :]
-    node_base = dot(my_mesh.astype(BF16), nw1[:width, :]) + vec_ref[4:5, :]
+    node_base = dot(my_mesh.astype(BF16), nw1[:width, :]) + nb1_ref[...]
 
     fwd_copies = [fwd_copy(i) for i in range(CHUNKS)]
     for i in range(CHUNKS):
@@ -244,9 +258,9 @@
         copy.wait_recv()
     gather(1, 1 - h)
 
-    b2 = vec_ref[1:2, :]
-    gain = vec_ref[2:3, :]
-    shift = vec_ref[3:4, :]
+    b2 = b2_ref[...]
+    gain = gain_ref[...]
+    shift = shift_ref[...]
     total[...] = jnp.zeros_like(total)
     node_row = lax.broadcasted_iota(jnp.int32, (mesh_rows, quart), 0)
 
@@ -264,7 +278,11 @@
         hidden = base[rows, :] + dot(arrived[0, s], w1[low, :]) + dot(arrived[1, s], w1[high, :])
         update = dot(silu(hidden).astype(BF16), w2[...]) + b2
         fresh = (edge[rows, :].astype(F32) + normalize(update, gain, shift)).astype(BF16)
-        hit = jnp.where(node_row == dst_ref[pl.ds(s, 1), :], 1.0, 0.0).astype(BF16)
+        if aligned:
+            targets = dst_wide[:, rows]
+        else:
+            targets = dst_ref[pl.ds(s, 1), :]
+        hit = jnp.where(node_row == targets, 1.0, 0.0).astype(BF16)
         total[...] += dot(hit, fresh)
         return carry
 
@@ -285,8 +303,8 @@
         sum_copies[k - 1].wait_recv()
         summed = summed + part_in[k - 1].astype(F32)
     hidden = node_base + dot(summed.astype(BF16), nw1[width:, :])
-    update = dot(silu(hidden).astype(BF16), nw2[...]) + vec_ref[5:6, :]
-    fresh = (my_mesh + normalize(update, vec_ref[6:7, :], vec_ref[7:8, :])).astype(BF16)
+    update = dot(silu(hidden).astype(BF16), nw2[...]) + nb2_ref[...]
+    fresh = (my_mesh + normalize(update, ngain_ref[...], nshift_ref[...])).astype(BF16)
     for k in range(nf):
         cols_out[k] = fresh[:, k * quarter : (k + 1) * quarter]
     out_copies = []
@@ -343,19 +361,22 @@
     slots = edges.shape[0]
     quart = slots // n
     hidden = edge_w1.shape[1]
-    own_src = lax.dynamic_slice_in_dim(
-        edge_src.reshape(n, nf, quart), lax.axis_index("feat"), 1, 1
-    ).reshape(-1, LANES)
-    vectors = jnp.stack(
-        [edge_b1, edge_b2, edge_gain, edge_shift, node_b1, node_b2, node_gain, node_shift]
-    )
+    targets = edge_dst.reshape(1, slots)
+    if quart % LANES == 0:
+        sources, grouped = edge_src, targets
+    else:
+        sources = lax.dynamic_slice_in_dim(
+            edge_src.reshape(n, nf, quart), lax.axis_index("feat"), 1, 1
+        ).reshape(1, slots)
+        grouped = edge_dst.reshape(n, quart)
+    vectors = (edge_b1, edge_b2, edge_gain, edge_shift, node_b1, node_b2, node_gain, node_shift)
     vmem = pl.BlockSpec(memory_space=pltpu.VMEM)
     anyspace = pl.BlockSpec(memory_space=pl.ANY)
     dma = pltpu.SemaphoreType.DMA
     return pl.pallas_call(
         functools.partial(kernel, n, nf),
         out_shape=jax.ShapeDtypeStruct((mesh_rows, quarter), BF16),
-        in_specs=[vmem] * 6 + [anyspace] * 5,
+        in_specs=[vmem] * 13 + [anyspace] * 5,
         out_specs=vmem,
         scratch_shapes=[
             pltpu.VMEM((slots, width), BF16),
@@ -397,10 +418,10 @@
     )(
         grid_latent,
         mesh_latent,
-        own_src,
-        edge_dst.reshape(n, quart),
-        edge_dst.reshape(-1, LANES),
-        vectors,
+        sources,
+        grouped,
+        targets,
+        *(v.reshape(1, -1) for v in vectors),
         edges,
         edge_w1,
         edge_w2,

time: 72.9 us -> 66.9 us (0.918)
  local copies, waits for them, and re-layouts: 4.56 us -> 1.4 us
  other arithmetic: 2.84 us -> 0 us
    unnamed x2 -> x0, other arithmetic: 2.84 us -> none
    another operation x1 -> x0, local copies, waits for them, and re-layouts: 1.42 us -> none  [body(): jnp.stack([edge_b1, edge_b2, edge_gain, edge_shift, node_b1, node_b2, nod...]
    unnamed x2 -> x1, local copies, waits for them, and re-layouts: 1.91 us -> 1.4 us
where the time goes in v2:
time: 66.9 us; the launch traced here: 66.7 us
  Pallas kernels  65.3 us (98%)
  local copies, waits for them, and re-layouts  1.4 us (2%)
    pallas_call x1, Pallas kernels, body(): pl.pallas_call(functools.partial(kernel, n, nf), out_shape=jax.ShapeDtype...  65.3 us
    unnamed x1, local copies, waits for them, and re-layouts  1.4 us

profile of v2, /device:TPU:29, one launch (start us, length us, event | category | flops | bytes accessed | tf_op | source)
XLA Modules:
  0.0 66.7 jit_solution(1323707110647364972)
XLA Ops:
  0.0 65.3 %encoder_step.1 = bf16[160,128]{1,0:T(8,128)(2,1)} custom-call(bf16[2048,128]{1,0:T(8,128)(2,1)} %grid_ref.1, bf16[160,128]{1,0:T(8,128)(2,1)} %mesh_ref.1, s32[1,8192]{1,0:T(1,128)} %src_ref.1, s32[1,2048]{1,0:T(1,128)} %bitcast.11, s32[1,2048]{1,0:T(1,128)} %bitcast.12, f32[1,512]{1,0:T(1,128)} %bitcast.13, f32[1,512]{1,0:T(1,128)} %bitcast.14, ...), custom_call_target="tpu_custom_call" | custom-call | tf_op jit(solution)/shard_map/encoder_step/pallas_call | solution.py:376
  65.3 1.4 %copy.19 = bf16[160,128]{1,0:T(8,128)(2,1)} copy(bf16[160,128]{1,0:T(8,128)(2,1)} %encoder_step.1) | data formatting | bytes 81920
